TPU v7x, 32 devices: a whole 2x2x4 slice. The times are simulated.
32 devices in a mesh: bank: 4 (over x, core), zero: 8 (over z, y).
Axes of the slice: x: 2, y: 2, z: 4, core: 2. Of those that a mesh axis runs over, the one named last changes fastest.
Arguments:
- train_gate: float32 [128, 2048, 768], P('bank', 'zero'), may hold values from -0.1875 to 0.1875
- other_gate: bfloat16 [128, 2048, 768], P('bank', 'zero'), may hold values from -0.0625 to 0.0625
- train_up: float32 [128, 2048, 768], P('bank', 'zero'), may hold values from -0.1875 to 0.1875
- other_up: bfloat16 [128, 2048, 768], P('bank', 'zero'), may hold values from -0.0625 to 0.0625
- router_weight: float32 [2048, 128], P('zero', 'bank'), may hold values from -0.125 to 0.125
- router_gain: float32 [2048], P('zero'), may hold values from 0.25 to 1.75
Outputs:
- ready_gate: bfloat16 [128, 2048, 768], P('bank', None, 'zero')
- ready_up: bfloat16 [128, 2048, 768], P('bank', None, 'zero')
- scale_gate: float32 [128, 768], P('bank', 'zero')
- scale_up: float32 [128, 768], P('bank', 'zero')
- serve_router: bfloat16 [2048, 128], replicated
All inputs are finite; a program needn't handle non-finite values. Where the computation divides by a largest or mean magnitude, that divisor is 1e-20 or more.
Results may differ from a plain program's by a relative error of at most 0.001.
Values may be sent and summed in bfloat16 or wider, within the bound.
No kernel may reach another device: no remote copies, remote signals or barrier semaphores. Data moves between devices by JAX's collectives and lax.ppermute only.
A program may use at most 256 MiB of HBM per device.

v0:
```python
import jax
import jax.numpy as jnp
from jax import lax
from jax.sharding import PartitionSpec as P


def on_device(train_gate, other_gate, train_up, other_up, router_weight, router_gain):
    latest_gate = train_gate + other_gate.astype(jnp.float32)
    latest_up = train_up + other_up.astype(jnp.float32)
    scale_gate, scale_up = lax.pmax(
        (jnp.max(jnp.abs(latest_gate), axis=1), jnp.max(jnp.abs(latest_up), axis=1)), "zero"
    )
    narrow_gate, narrow_up = (
        (latest_gate / jnp.expand_dims(scale_gate, 1)).astype(jnp.bfloat16),
        (latest_up / jnp.expand_dims(scale_up, 1)).astype(jnp.bfloat16),
    )
    ready_gate, ready_up = (
        lax.all_to_all(narrow_gate, "zero", split_axis=2, concat_axis=1, tiled=True),
        lax.all_to_all(narrow_up, "zero", split_axis=2, concat_axis=1, tiled=True),
    )
    scale_gate = lax.dynamic_slice_in_dim(
        scale_gate, lax.axis_index("zero") * ready_gate.shape[2], ready_gate.shape[2], axis=1
    )
    scale_up = lax.dynamic_slice_in_dim(
        scale_up, lax.axis_index("zero") * ready_up.shape[2], ready_up.shape[2], axis=1
    )
    part_router = (router_weight * router_gain[:, None]).astype(jnp.bfloat16)
    row_router = lax.all_gather(part_router, "zero", axis=0, tiled=True)
    serve_router = lax.all_gather(row_router, "bank", axis=1, tiled=True)
    return (ready_gate, ready_up, scale_gate, scale_up, serve_router)


def solution(mesh):
    return jax.shard_map(
        on_device,
        mesh=mesh,
        in_specs=(
            P("bank", "zero", None),
            P("bank", "zero", None),
            P("bank", "zero", None),
            P("bank", "zero", None),
            P("zero", "bank"),
            P("zero"),
        ),
        out_specs=(
            P("bank", None, "zero"),
            P("bank", None, "zero"),
            P("bank", "zero"),
            P("bank", "zero"),
            P(),
        ),
        check_vma=False,
    )
```

profile of v0, /device:TPU:0, one launch (start us, length us, event | category | flops | bytes accessed | tf_op | source)
XLA Modules:
  0.0 885.5 jit_solution(4941322030642369728)
XLA Ops:
  7.2 0.0 all-reduce.3.cloned.1.call-start
  7.2 25.0 %copy.42 = f32[32,256,768]{1,0,2:T(8,128)} copy(f32[32,256,768]{2,1,0:T(8,128)} %param.8) | data formatting | bytes 50331648 | tf_op args[2]
  32.2 16.9 %copy.41 = bf16[32,256,768]{1,0,2:T(8,128)(2,1)} copy(bf16[32,256,768]{2,1,0:T(8,128)(2,1)} %param.9) | data formatting | bytes 25165824 | tf_op args[3]
  49.1 25.0 %copy.38 = f32[32,256,768]{1,0,2:T(8,128)} copy(f32[32,256,768]{2,1,0:T(8,128)} %param.6) | data formatting | bytes 50331648 | tf_op args[0]
  74.2 16.9 %copy.37 = bf16[32,256,768]{1,0,2:T(8,128)(2,1)} copy(bf16[32,256,768]{2,1,0:T(8,128)(2,1)} %param.7) | data formatting | bytes 25165824 | tf_op args[1]
  91.0 0.0 copy-start
  91.0 14.4 %abs_reduce_fusion = f32[32,768]{0,1:T(8,128)} fusion(f32[32,256,768]{1,0,2:T(8,128)} %copy.42, bf16[32,256,768]{1,0,2:T(8,128)(2,1)} %copy.41), kind=kLoop, calls=%fused_computation.1 | loop fusion | flops 25141248 | bytes 37847040 | tf_op jit(solution)/shard_map/reduce_max | solution.py:11
  105.4 4.7 copy-done
  110.1 9.7 %abs_reduce_fusion.1 = f32[32,768]{0,1:T(8,128)} fusion(f32[32,256,768]{1,0,2:T(8,128)S(1)} %copy-done, bf16[32,256,768]{1,0,2:T(8,128)(2,1)} %copy.37), kind=kLoop, calls=%fused_computation.4 | loop fusion | flops 25141248 | bytes 37847040 | tf_op jit(solution)/shard_map/reduce_max | solution.py:11
  119.9 0.0 all-reduce.3.cloned.1.call-update
  119.9 78.2 %all-reduce.3.cloned.1.call-done = (f32[32,768]{0,1:T(8,128)}, f32[32,768]{0,1:T(8,128)}) async-done(((f32[32,768]{0,1:T(8,128)}, f32[32,768]{0,1:T(8,128)}), (f32[32,768]{0,1:T(8,128)}, f32[32,768]{0,1:T(8,128)})) %all-reduce.3.cloned.1.call-update) | async-done | bytes 196624 | tf_op jit(solution)/shard_map/pmax | solution.py:10
  198.1 29.4 %divide_convert_fusion = (bf16[32,256,768]{1,0,2:T(8,128)(2,1)}, bf16[32,256,768]{1,0,2:T(8,128)(2,1)S(1)}) fusion(f32[32,256,768]{1,0,2:T(8,128)} %copy.42, bf16[32,256,768]{1,0,2:T(8,128)(2,1)} %copy.41, f32[32,768]{0,1:T(8,128)} %get-tuple-element.16, f32[32,768]{0,1:T(8,128)} %get-tuple-element.15, f32[32,256,768]{1,0,2:T(8,128)} %copy.38, ...), kind=kLoop, calls=%fused_computation | loop fusion | flops 50331648 | bytes 100859904 | tf_op jit(solution)/shard_map/convert_element_type | solution.py:15
  227.5 0.0 copy-start.1
  227.6 0.0 copy-start.2
  227.6 276.4 %all_to_all.36 = bf16[32,256,768]{1,0,2:T(8,128)(2,1)} all-to-all(bf16[32,256,768]{1,0,2:T(8,128)(2,1)S(1)} %get-tuple-element.18), channel_id=1, replica_groups=mesh['bank'=4,'zero'=8] {'zero'}, dimensions={2} | all-to-all | bytes 25165824 | tf_op jit(solution)/shard_map/all_to_all | solution.py:18
  504.0 5.4 all-to-all-start.1
  509.3 0.0 copy-done.1
  509.4 0.0 copy-done.2
  509.4 292.0 %all_gather.6 = bf16[2048,32]{0,1:T(8,128)(2,1)S(1)} all-gather(bf16[256,32]{0,1:T(8,128)(2,1)S(1)} %multiply_convert_fusion), channel_id=1, replica_groups=mesh['bank'=4,'zero'=8] {'zero'}, dimensions={0}, use_global_device_ids=true | all-gather | bytes 147456 | tf_op jit(solution)/shard_map/all_gather | solution.py:28
  801.4 7.0 all_gather.7
  808.4 1.0 copy.47
  809.4 0.8 constant_dynamic-slice_fusion
  810.2 0.7 copy.45
  810.9 0.7 copy.46
  811.6 14.1 %copy.40 = bf16[32,8,256,96]{2,1,3,0:T(8,128)(2,1)} copy(bf16[32,8,256,96]{2,0,3,1:T(8,128)(2,1)} %bitcast.14) | data formatting | bytes 25165824 | tf_op jit(solution)/shard_map/all_to_all | solution.py:18
  825.6 19.5 %all_to_all.29 = bf16[32,2048,96]{1,2,0:T(8,128)(2,1)} reshape(bf16[32,8,256,96]{2,1,3,0:T(8,128)(2,1)} %copy.40) | data formatting | bytes 25165824 | tf_op jit(solution)/shard_map/all_to_all | solution.py:18
  845.1 0.0 all-to-all-done.1
  845.1 14.1 %copy.44 = bf16[32,8,256,96]{2,1,3,0:T(8,128)(2,1)} copy(bf16[32,8,256,96]{2,0,3,1:T(8,128)(2,1)} %bitcast.5) | data formatting | bytes 25165824 | tf_op jit(solution)/shard_map/all_to_all | solution.py:19
  859.2 19.5 %all_to_all.33 = bf16[32,2048,96]{1,2,0:T(8,128)(2,1)} reshape(bf16[32,8,256,96]{2,1,3,0:T(8,128)(2,1)} %copy.44) | data formatting | bytes 25165824 | tf_op jit(solution)/shard_map/all_to_all | solution.py:19
  (1 shorter events, 0.0 us)
Async XLA Ops:
  7.2 191.0 %all-reduce.3.cloned.1.call-start = ((), (), s32[]{:S(2)}) async-start(), calls=%async_computation.2 | async-start | bytes 1572864 | tf_op jit(solution)/shard_map/pmax | solution.py:10
  91.0 19.1 %copy-start = (f32[32,256,768]{1,0,2:T(8,128)S(1)}, f32[32,256,768]{1,0,2:T(8,128)}, u32[]{:S(2)}) copy-start(f32[32,256,768]{1,0,2:T(8,128)} %copy.38) | copy-start | bytes 75497472
  227.5 281.8 %copy-start.1 = (f32[256,32]{0,1:T(8,128)S(1)}, f32[256,32]{0,1:T(8,128)}, u32[]{:S(2)}) copy-start(f32[256,32]{0,1:T(8,128)} %param.10) | copy-start | bytes 98308
  227.6 281.8 %copy-start.2 = (f32[256]{0:T(256)S(1)}, f32[256]{0:T(256)}, u32[]{:S(2)}) copy-start(f32[256]{0:T(256)} %param.11) | copy-start | bytes 3076
  504.0 341.1 %all-to-all-start.1 = ((bf16[32,256,768]{1,0,2:T(8,128)(2,1)}), bf16[32,256,768]{1,0,2:T(8,128)(2,1)}, u32[]{:S(2)}, u32[]{:S(2)}) async-start(bf16[32,256,768]{1,0,2:T(8,128)(2,1)} %get-tuple-element.17), calls=%async_computation.1 | async-start | bytes 25165824 | tf_op jit(solution)/shard_map/all_to_all | solution.py:19
Sparse Core Ops, SparseCore 0:
  120.0 78.0 all-reduce.2
where the time goes:
time: 889 us; the launch traced here: 886 us
  blocking collectives  575 us (65%)
  local copies, waits for them, and re-layouts  159 us (18%)
  waiting for transfers between devices  78.2 us (9%)
  other arithmetic  53.5 us (6%)
  between operations  14.1 us (2%)
    all_gather x1, blocking collectives, on_device(): row_router = lax.all_gather(part_router, 'zero', axis=0, tiled=True)  292 us
    all_to_all x1, blocking collectives, on_device(): lax.all_to_all(narrow_gate, 'zero', split_axis=2, concat_axis=1, tiled=True)  276 us
    unnamed x13, local copies, waits for them, and re-layouts  90.9 us
    pmax x1, waiting for transfers between devices, on_device(): lax.pmax((jnp.max(jnp.abs(latest_gate), axis=1), jnp.max(jnp.abs(latest_u...  78.2 us
    all_to_all x2, local copies, waits for them, and re-layouts, on_device(): lax.all_to_all(narrow_gate, 'zero', split_axis=2, concat_axis=1, tiled=True)  33.5 us
    all_to_all x2, local copies, waits for them, and re-layouts, on_device(): lax.all_to_all(narrow_up, 'zero', split_axis=2, concat_axis=1, tiled=True)  33.5 us
    convert_element_type x1, other arithmetic, on_device(): (latest_up / jnp.expand_dims(scale_up, 1)).astype(jnp.bfloat16)  29.4 us
  transfers between devices with their start and end apart: 2, of which 1 were waited for; matrix products, arithmetic and copies ran while one was open for 2% of the time, Pallas kernels for 0%

commit v1 on v0

v1 whole, which is shorter than its diff:
```python
import functools

import jax
import jax.numpy as jnp
from jax import lax
from jax.experimental import pallas as pl
from jax.experimental.pallas import tpu as pltpu
from jax.sharding import PartitionSpec as P

VMEM_LIMIT = 48 * 1024 * 1024


def cost(flops, moved):
    return pl.CostEstimate(flops=flops, bytes_accessed=moved, transcendentals=0)


def max_kernel(train_ref, other_ref, out_ref):
    latest = train_ref[...] + other_ref[...].astype(jnp.float32)
    out_ref[...] = jnp.max(jnp.abs(latest), axis=1, keepdims=True)


def column_max(train, other, first, count):
    _, rows, columns = train.shape
    step = 4 if count % 4 == 0 and first % 4 == 0 else 1
    at = lambda i: (first // step + i, 0, 0)
    return pl.pallas_call(
        max_kernel,
        grid=(count // step,),
        in_specs=[pl.BlockSpec((step, rows, columns), at)] * 2,
        out_specs=pl.BlockSpec((step, 1, columns), lambda i: (i, 0, 0)),
        out_shape=jax.ShapeDtypeStruct((count, 1, columns), jnp.float32),
        cost_estimate=cost(count * rows * columns * 60, count * rows * columns * 6),
        compiler_params=pltpu.CompilerParams(vmem_limit_bytes=VMEM_LIMIT),
        name="column_max",
    )(train, other)


def narrow_kernel(parts, train_ref, other_ref, scale_ref, out_ref):
    for e in range(train_ref.shape[0]):
        latest = train_ref[e] + other_ref[e].astype(jnp.float32)
        turned = (latest / scale_ref[e]).T
        width = turned.shape[0] // parts
        for d in range(parts):
            out_ref[d, e] = turned[d * width : (d + 1) * width].astype(jnp.bfloat16)


def narrow(train, other, scale, first, count, parts):
    _, rows, columns = train.shape
    step = 2 if count % 2 == 0 and first % 2 == 0 else 1
    at = lambda i: (first // step + i, 0, 0)
    return pl.pallas_call(
        functools.partial(narrow_kernel, parts),
        grid=(count // step,),
        in_specs=[pl.BlockSpec((step, rows, columns), at)] * 2
        + [pl.BlockSpec((step, 1, columns), lambda i: (i, 0, 0))],
        out_specs=pl.BlockSpec((parts, step, columns // parts, rows), lambda i: (0, i, 0, 0)),
        out_shape=jax.ShapeDtypeStruct((parts, count, columns // parts, rows), jnp.bfloat16),
        cost_estimate=cost(count * rows * columns * 100, count * rows * columns * 8),
        compiler_params=pltpu.CompilerParams(vmem_limit_bytes=VMEM_LIMIT),
        name="narrow",
    )(train, other, scale)


def place_kernel(in_ref, *refs):
    out_ref = refs[-1]
    rows = in_ref.shape[3]
    for s in range(in_ref.shape[0]):
        out_ref[:, :, s * rows : (s + 1) * rows] = in_ref[s]


def place(received, held, first, experts):
    parts, count, width, rows = received.shape
    step = 2 if count % 2 == 0 and first % 2 == 0 else 1
    specs = [pl.BlockSpec((parts, step, width, rows), lambda i: (0, i, 0, 0))]
    args = [received]
    if held is not None:
        specs.append(pl.BlockSpec(memory_space=pl.ANY))
        args.append(held)
    return pl.pallas_call(
        place_kernel,
        grid=(count // step,),
        in_specs=specs,
        out_specs=pl.BlockSpec((step, width, parts * rows), lambda i: (first // step + i, 0, 0)),
        out_shape=jax.ShapeDtypeStruct((experts, width, parts * rows), jnp.bfloat16),
        input_output_aliases={} if held is None else {1: 0},
        cost_estimate=cost(parts * count * width * rows * 40, parts * count * width * rows * 4),
        compiler_params=pltpu.CompilerParams(vmem_limit_bytes=VMEM_LIMIT),
        name="place",
    )(*args)


def route(router_weight, router_gain):
    part = (router_weight * router_gain[:, None]).astype(jnp.bfloat16)
    row = lax.all_gather(part, "zero", axis=0, tiled=True)
    return lax.all_gather(row, "bank", axis=1, tiled=True)


def plain(train_gate, other_gate, train_up, other_up, router_weight, router_gain):
    latest = [t + o.astype(jnp.float32) for t, o in ((train_gate, other_gate), (train_up, other_up))]
    scales = lax.pmax([jnp.max(jnp.abs(a), axis=1) for a in latest], "zero")
    ready, own = [], []
    for a, s in zip(latest, scales):
        thin = (a / s[:, None]).astype(jnp.bfloat16)
        ready.append(lax.all_to_all(thin, "zero", split_axis=2, concat_axis=1, tiled=True))
        width = ready[-1].shape[2]
        own.append(lax.dynamic_slice_in_dim(s, lax.axis_index("zero") * width, width, axis=1))
    return (*ready, *own, route(router_weight, router_gain))


def chunked(parts, train_gate, other_gate, train_up, other_up, router_weight, router_gain):
    pairs = ((train_gate, other_gate), (train_up, other_up))
    experts, rows, columns = train_gate.shape
    half, lead = experts // 2, experts // 4 * 3
    chunks = ((0, 0, lead), (0, lead, experts - lead), (1, 0, half), (1, half, half))
    width = columns // parts

    def exchange(block):
        return lax.all_to_all(block, "zero", split_axis=0, concat_axis=0, tiled=True)

    scale = [None] * len(chunks)
    own_max = column_max(*pairs[0], 0, lead)
    scale[0] = jnp.max(lax.all_gather(own_max, "zero"), axis=0)
    thin = [narrow(*pairs[0], scale[0], 0, lead, parts)]
    later, _ = lax.optimization_barrier((pairs, thin[0]))
    rest = [column_max(*later[t], f, c) for t, f, c in chunks[1:]]
    scale[1:] = lax.pmax(rest, "zero")
    got = [exchange(thin[0])]
    for k in range(1, len(chunks)):
        t, f, c = chunks[k]
        thin.append(narrow(*pairs[t], scale[k], f, c, parts))
        if k == 2:
            router_weight, _ = lax.optimization_barrier((router_weight, thin[k]))
            serve_router = route(router_weight, router_gain)
            thin[k], serve_router = lax.optimization_barrier((thin[k], serve_router))
        block, _ = lax.optimization_barrier((thin[k], got[k - 1]))
        got.append(exchange(block))
    ready, own = [], []
    for t in range(2):
        held = None
        for k, (u, f, c) in enumerate(chunks):
            if u == t:
                held = place(got[k], held, f, experts)
        ready.append(jnp.swapaxes(held, 1, 2))
        both = jnp.concatenate([scale[k][:, 0] for k, (u, _, _) in enumerate(chunks) if u == t])
        own.append(lax.dynamic_slice_in_dim(both, lax.axis_index("zero") * width, width, axis=1))
    return (*ready, *own, serve_router)


def solution(mesh):
    parts = mesh.shape["zero"]

    def on_device(train_gate, *others):
        experts, rows, columns = train_gate.shape
        if rows % 128 == 0 and columns % (16 * parts) == 0 and experts % 4 == 0:
            return chunked(parts, train_gate, *others)
        return plain(train_gate, *others)

    return jax.shard_map(
        on_device,
        mesh=mesh,
        in_specs=(
            P("bank", "zero", None),
            P("bank", "zero", None),
            P("bank", "zero", None),
            P("bank", "zero", None),
            P("zero", "bank"),
            P("zero"),
        ),
        out_specs=(
            P("bank", None, "zero"),
            P("bank", None, "zero"),
            P("bank", "zero"),
            P("bank", "zero"),
            P(),
        ),
        check_vma=False,
    )
```

time: 889 us -> 708 us (0.80)
  blocking collectives: 575 us -> 119 us
  waiting for transfers between devices: 78.2 us -> 444 us
  local copies, waits for them, and re-layouts: 159 us -> 5.24 us
  Pallas kernels: 0 us -> 103 us
  other arithmetic: 53.5 us -> 0.73 us
  starting transfers between devices: 5.39 us -> 19.8 us
    all_to_all x1 -> x0, blocking collectives: 276 us -> none  [on_device(): lax.all_to_all(narrow_gate, 'zero', split_axis=2, concat_axis=1, tiled=True)]
    all_to_all x1 -> x4, waiting for transfers between devices: 0.01 us -> 241 us  [exchange(): lax.all_to_all(block, 'zero', split_axis=0, concat_axis=0, tiled=True)]
    all_gather x2 -> x3, blocking collectives: 299 us -> 119 us  [the longest x1 77.9 us: route(): row = lax.all_gather(part, 'zero', axis=0, tiled=True)]
    pmax x1, waiting for transfers between devices: 78.2 us -> 204 us  [chunked(): scale[1:] = lax.pmax(rest, 'zero')]
    pallas_call x0 -> x12, Pallas kernels: none -> 103 us  [the longest x4 44 us: narrow(): pl.pallas_call(functools.partial(narrow_kernel, parts), grid=(count // st...]
    unnamed x13 -> x18, local copies, waits for them, and re-layouts: 90.9 us -> 4.51 us
    all_to_all x4 -> x0, local copies, waits for them, and re-layouts: 67.1 us -> none  [the longest x2 33.5 us: on_device(): lax.all_to_all(narrow_gate, 'zero', split_axis=2, concat_axis=1, tiled=True)]
    convert_element_type x2 -> x1, other arithmetic: 29.4 us -> 0.01 us  [route(): part = (router_weight * router_gain[:, None]).astype(jnp.bfloat16)]
  transfers between devices with their start and end apart: 2 -> 5, of which waited for: 1 -> 3; matrix products, arithmetic and copies ran while one was open for 2% -> 0% of each run, Pallas kernels for 0% -> 10%
where the time goes in v1:
time: 708 us; the launch traced here: 706 us
  waiting for transfers between devices  444 us (63%)
  blocking collectives  119 us (17%)
  Pallas kernels  103 us (15%)
  starting transfers between devices  19.8 us (3%)
  between operations  14.2 us (2%)
    all_to_all x4, waiting for transfers between devices, exchange(): lax.all_to_all(block, 'zero', split_axis=0, concat_axis=0, tiled=True)  241 us
    pmax x1, waiting for transfers between devices, chunked(): scale[1:] = lax.pmax(rest, 'zero')  204 us
    all_gather x1, blocking collectives, route(): row = lax.all_gather(part, 'zero', axis=0, tiled=True)  77.9 us
    pallas_call x4, Pallas kernels, narrow(): pl.pallas_call(functools.partial(narrow_kernel, parts), grid=(count // st...  44 us
    all_gather x1, blocking collectives, chunked(): scale[0] = jnp.max(lax.all_gather(own_max, 'zero'), axis=0)  33.3 us
    pallas_call x4, Pallas kernels, place(): pl.pallas_call(place_kernel, grid=(count // step,), in_specs=specs, out_s...  29.9 us
    pallas_call x4, Pallas kernels, column_max(): pl.pallas_call(max_kernel, grid=(count // step,), in_specs=[pl.BlockSpec(...  29 us
    all_to_all x4, starting transfers between devices, exchange(): lax.all_to_all(block, 'zero', split_axis=0, concat_axis=0, tiled=True)  19.8 us
  transfers between devices with their start and end apart: 5, of which 3 were waited for; matrix products, arithmetic and copies ran while one was open for 0% of the time, Pallas kernels for 10%

profile of v1, /device:TPU:0, one launch (start us, length us, event | category | flops | bytes accessed | tf_op | source)
XLA Modules:
  0.0 706.0 jit_solution(13248146906254693145)
XLA Ops:
  7.2 9.8 %column_max.4 = f32[24,1,768]{2,1,0:T(1,128)S(1)} custom-call(f32[32,256,768]{2,1,0:T(8,128)} %train_ref.8, bf16[32,256,768]{2,1,0:T(8,128)(2,1)} %other_ref.8), custom_call_target="tpu_custom_call" | custom-call | flops 283115520 | bytes 28311552 | tf_op jit(solution)/shard_map/column_max/pallas_call | solution.py:26
  17.0 33.3 %all-gather = f32[192,1,768]{2,1,0:T(1,128)S(1)} all-gather(f32[24,1,768]{2,1,0:T(1,128)S(1)} %column_max.4), channel_id=2, replica_groups=mesh['bank'=4,'zero'=8] {'zero'}, dimensions={0}, use_global_device_ids=true | all-gather | bytes 663552 | tf_op jit(solution)/shard_map/all_gather | solution.py:122
  50.3 0.1 reduce_max.12.scale_ref
  50.4 16.5 %narrow.4 = bf16[8,24,96,256]{3,2,1,0:T(8,128)(2,1)} custom-call(f32[32,256,768]{2,1,0:T(8,128)} %train_ref.8, bf16[32,256,768]{2,1,0:T(8,128)(2,1)} %other_ref.8, f32[24,1,768]{2,1,0:T(1,128)S(1)} %reduce_max.12.scale_ref), custom_call_target="tpu_custom_call" | custom-call | flops 471859200 | bytes 37748736 | tf_op jit(solution)/shard_map/narrow/pallas_call | solution.py:51
  66.9 5.6 all-to-all-start
  72.5 0.0 all-reduce.3.cloned.1.call-start
  72.5 7.0 column_max.6
  79.5 0.6 copy.16
  80.2 4.6 column_max.5
  84.8 7.6 %column_max.7 = f32[16,1,768]{2,1,0:T(1,128)} custom-call(f32[32,256,768]{2,1,0:T(8,128)} %train_ref.12, bf16[32,256,768]{2,1,0:T(8,128)(2,1)} %other_ref.12), custom_call_target="tpu_custom_call" | custom-call | flops 188743680 | bytes 18874368 | tf_op jit(solution)/shard_map/column_max/pallas_call | solution.py:26
  92.3 0.0 all-reduce.3.cloned.1.call-update
  92.4 203.5 %all-reduce.3.cloned.1.call-done = (f32[8,1,768]{2,1,0:T(1,128)}, f32[16,1,768]{2,0,1:T(8,128)}, f32[16,1,768]{2,1,0:T(1,128)}) async-done(((f32[8,1,768]{2,1,0:T(1,128)}, f32[16,1,768]{2,0,1:T(8,128)}, f32[16,1,768]{2,1,0:T(1,128)}), (f32[8,1,768]{2,1,0:T(1,128)}, f32[16,1,768]{2,0,1:T(8,128)}, f32[16,1,768]{2,1,0:T(1,128)})) %all-reduce.3.cloned.1.call-update) | async-done | bytes 122896 | tf_op jit(solution)/shard_map/pmax | solution.py:126
  295.9 0.7 copy-done.2
  296.6 4.9 narrow.5
  301.5 0.0 copy-start
  301.6 1.7 copy-done
  303.2 4.6 all-to-all-start.1
  307.9 11.3 %narrow.7 = bf16[8,16,96,256]{3,2,1,0:T(8,128)(2,1)} custom-call(f32[32,256,768]{2,1,0:T(8,128)} %train_ref.12, bf16[32,256,768]{2,1,0:T(8,128)(2,1)} %other_ref.12, f32[16,1,768]{2,1,0:T(1,128)S(1)} %copy-done.1), custom_call_target="tpu_custom_call" | custom-call | flops 314572800 | bytes 25165824 | tf_op jit(solution)/shard_map/narrow/pallas_call | solution.py:51
  319.2 77.9 %all_gather.14 = bf16[2048,32]{0,1:T(8,128)(2,1)S(1)} all-gather(bf16[256,32]{0,1:T(8,128)(2,1)S(1)} %multiply_convert_fusion), channel_id=1, replica_groups=mesh['bank'=4,'zero'=8] {'zero'}, dimensions={0}, use_global_device_ids=true | all-gather | bytes 147456 | tf_op jit(solution)/shard_map/all_gather | solution.py:94
  397.1 7.6 %all_gather.15 = bf16[2048,128]{0,1:T(8,128)(2,1)} all-gather(bf16[2048,32]{0,1:T(8,128)(2,1)S(1)} %all_gather.14), channel_id=1, replica_groups=mesh['bank'=4,'zero'=8] {'bank'}, dimensions={1}, use_global_device_ids=true | all-gather | bytes 655360 | tf_op jit(solution)/shard_map/all_gather | solution.py:95
  404.7 4.8 all-to-all-start.2
  409.4 0.1 copy.17.scale_ref
  409.5 11.3 %narrow.6 = bf16[8,16,96,256]{3,2,1,0:T(8,128)(2,1)} custom-call(f32[32,256,768]{2,1,0:T(8,128)} %train_ref.12, bf16[32,256,768]{2,1,0:T(8,128)(2,1)} %other_ref.12, f32[16,1,768]{2,1,0:T(1,128)S(1)} %copy.17.scale_ref), custom_call_target="tpu_custom_call" | custom-call | flops 314572800 | bytes 25165824 | tf_op jit(solution)/shard_map/narrow/pallas_call | solution.py:51
  420.8 127.5 %all-to-all-done.2.in_ref = bf16[8,16,96,256]{3,2,1,0:T(8,128)(2,1)} async-done(((bf16[8,16,96,256]{3,2,1,0:T(8,128)(2,1)}), bf16[8,16,96,256]{3,2,1,0:T(8,128)(2,1)}, u32[]{:S(2)}, u32[]{:S(2)}) %all-to-all-start.2) | async-done | bytes 6291488 | tf_op jit(solution)/shard_map/all_to_all | solution.py:118
  548.4 4.8 all-to-all-start.3
  553.2 2.0 copy.18
  555.2 0.7 fusion
  555.9 11.7 %place.4.refs_0_ = bf16[32,96,2048]{2,1,0:T(8,128)(2,1)} custom-call(bf16[8,24,96,256]{3,2,1,0:T(8,128)(2,1)} %all-to-all-done.in_ref), custom_call_target="tpu_custom_call" | custom-call | flops 188743680 | bytes 18874368 | tf_op jit(solution)/shard_map/place/pallas_call | solution.py:79
  567.6 2.4 place.5
  569.9 8.0 %place.6.refs_0_ = bf16[32,96,2048]{2,1,0:T(8,128)(2,1)} custom-call(bf16[8,16,96,256]{3,2,1,0:T(8,128)(2,1)} %all-to-all-done.2.in_ref), custom_call_target="tpu_custom_call" | custom-call | flops 125829120 | bytes 12582912 | tf_op jit(solution)/shard_map/place/pallas_call | solution.py:79
  577.9 113.3 %all-to-all-done.3.in_ref = bf16[8,16,96,256]{3,2,1,0:T(8,128)(2,1)} async-done(((bf16[8,16,96,256]{3,2,1,0:T(8,128)(2,1)}), bf16[8,16,96,256]{3,2,1,0:T(8,128)(2,1)}, u32[]{:S(2)}, u32[]{:S(2)}) %all-to-all-start.3) | async-done | bytes 6291488 | tf_op jit(solution)/shard_map/all_to_all | solution.py:118
  691.2 8.0 %place.7 = bf16[32,96,2048]{2,1,0:T(8,128)(2,1)} custom-call(bf16[8,16,96,256]{3,2,1,0:T(8,128)(2,1)} %all-to-all-done.3.in_ref, bf16[32,96,2048]{2,1,0:T(8,128)(2,1)} %place.6.refs_0_), custom_call_target="tpu_custom_call", output_to_operand_aliasing={{}: (1, {})} | custom-call | flops 125829120 | bytes 12582912 | tf_op jit(solution)/shard_map/place/pallas_call | solution.py:79
  (18 shorter events, 0.1 us)
Async XLA Ops:
  66.9 236.3 %all-to-all-start = ((bf16[8,24,96,256]{3,2,1,0:T(8,128)(2,1)}), bf16[8,24,96,256]{3,2,1,0:T(8,128)(2,1)}, u32[]{:S(2)}, u32[]{:S(2)}) async-start(bf16[8,24,96,256]{3,2,1,0:T(8,128)(2,1)} %narrow.4), calls=%async_computation | async-start | bytes 18874368 | tf_op jit(solution)/shard_map/all_to_all | solution.py:118
  72.5 223.4 %all-reduce.3.cloned.1.call-start = ((), (), s32[]{:S(2)}) async-start(), calls=%async_computation.4 | async-start | bytes 245760 | tf_op jit(solution)/shard_map/pmax | solution.py:126
  295.9 0.7 copy-start.2
  296.6 11.2 %copy-start.1 = (f32[16,1,768]{2,1,0:T(1,128)S(1)}, f32[16,1,768]{2,1,0:T(1,128)}, u32[]{:S(2)}) copy-start(f32[16,1,768]{2,1,0:T(1,128)} %get-tuple-element.32.scale_ref) | copy-start | bytes 147460
  301.5 1.7 copy-start
  303.2 101.5 %all-to-all-start.1 = ((bf16[8,8,96,256]{3,2,1,0:T(8,128)(2,1)}), bf16[8,8,96,256]{3,2,1,0:T(8,128)(2,1)S(1)}, u32[]{:S(2)}, u32[]{:S(2)}) async-start(bf16[8,8,96,256]{3,2,1,0:T(8,128)(2,1)} %copy-done), calls=%async_computation.1 | async-start | bytes 6291456 | tf_op jit(solution)/shard_map/all_to_all | solution.py:118
  307.8 11.3 %copy-start.5 = (f32[256,32]{0,1:T(8,128)S(1)}, f32[256,32]{0,1:T(8,128)}, u32[]{:S(2)}) copy-start(f32[256,32]{0,1:T(8,128)} %param.10) | copy-start | bytes 98308
  307.9 11.3 %copy-start.6 = (f32[256]{0:T(256)S(1)}, f32[256]{0:T(256)}, u32[]{:S(2)}) copy-start(f32[256]{0:T(256)} %param.11) | copy-start | bytes 3076
  319.2 90.3 %copy-start.4 = (f32[16,1,768]{2,0,1:T(8,128)S(1)}, f32[16,1,768]{2,0,1:T(8,128)}, u32[]{:S(2)}) copy-start(f32[16,1,768]{2,0,1:T(8,128)} %get-tuple-element.31) | copy-start | bytes 147460
  404.7 143.7 %all-to-all-start.2 = ((bf16[8,16,96,256]{3,2,1,0:T(8,128)(2,1)}), bf16[8,16,96,256]{3,2,1,0:T(8,128)(2,1)}, u32[]{:S(2)}, u32[]{:S(2)}) async-start(bf16[8,16,96,256]{3,2,1,0:T(8,128)(2,1)} %narrow.7), calls=%async_computation.2 | async-start | bytes 12582912 | tf_op jit(solution)/shard_map/all_to_all | solution.py:118
  420.8 132.3 %copy-start.3 = (f32[8,1,768]{2,1,0:T(1,128)S(1)}, f32[8,1,768]{2,1,0:T(1,128)}, u32[]{:S(2)}) copy-start(f32[8,1,768]{2,1,0:T(1,128)} %get-tuple-element.30.scale_ref) | copy-start | bytes 73732
  548.4 142.8 %all-to-all-start.3 = ((bf16[8,16,96,256]{3,2,1,0:T(8,128)(2,1)}), bf16[8,16,96,256]{3,2,1,0:T(8,128)(2,1)}, u32[]{:S(2)}, u32[]{:S(2)}) async-start(bf16[8,16,96,256]{3,2,1,0:T(8,128)(2,1)} %narrow.6), calls=%async_computation.3 | async-start | bytes 12582912 | tf_op jit(solution)/shard_map/all_to_all | solution.py:118
Sparse Core Ops, SparseCore 0:
  92.5 203.3 all-reduce.2
